TPU v7x, 32 devices: a whole 2x2x4 slice. The times are simulated.
32 devices in a mesh: dp: 4 (over z), hid: 2 (over x), dm: 4 (over y, core).
Axes of the slice: x: 2, y: 2, z: 4, core: 2. Of those that a mesh axis runs over, the one named last changes fastest.
Arguments:
- tokens: bfloat16 [32768, 1024], P(('dp', 'hid', 'dm')), may hold values from -6 to 6
- first_values: bfloat16 [32768, 1024], P(('dp', 'hid', 'dm')), may hold values from -6 to 6
- doc_lengths: int32 [32, 8], P(('dp', 'hid', 'dm')), may hold values from 1 to 512, 1024 in all within a row
- cotangent: bfloat16 [32768, 1024], P(('dp', 'hid', 'dm')), may hold values from -6 to 6
- attn_gain: bfloat16 [1024], P(('dp', 'hid', 'dm')), may hold values from 0.25 to 1.75
- w_query: bfloat16 [1024, 1024], P(('dp', 'hid', 'dm')), may hold values from -0.1875 to 0.1875
- w_key: bfloat16 [1024, 1024], P(('dp', 'hid', 'dm')), may hold values from -0.1875 to 0.1875
- w_value: bfloat16 [1024, 1024], P(('dp', 'hid', 'dm')), may hold values from -0.1875 to 0.1875
- w_out: bfloat16 [1024, 1024], P(('dp', 'hid', 'dm')), may hold values from -1 to 1
- mlp_gain: bfloat16 [1024], P(('dp', 'hid', 'dm')), may hold values from 0.25 to 1.75
- w_gate: bfloat16 [1024, 2816], P(None, ('hid', 'dm')), may hold values from -0.1875 to 0.1875
- w_up: bfloat16 [1024, 2816], P(None, ('hid', 'dm')), may hold values from -0.1875 to 0.1875
- w_down: bfloat16 [2816, 1024], P(('hid', 'dm')), may hold values from -0.109375 to 0.109375
Outputs:
- output: bfloat16 [32768, 1024], P(('dp', 'hid', 'dm'))
- tokens_grad: bfloat16 [32768, 1024], P(('dp', 'hid', 'dm'))
- first_values_grad: bfloat16 [32768, 1024], P(('dp', 'hid', 'dm'))
- w_query_grad: float32 [1024, 1024], P(('dp', 'hid', 'dm'))
- w_key_grad: float32 [1024, 1024], P(('dp', 'hid', 'dm'))
- w_value_grad: float32 [1024, 1024], P(('dp', 'hid', 'dm'))
- w_out_grad: float32 [1024, 1024], P(('dp', 'hid', 'dm'))
- attn_gain_grad: float32 [1024], P(('dp', 'hid', 'dm'))
- mlp_gain_grad: float32 [1024], P(('dp', 'hid', 'dm'))
- w_gate_grad: float32 [1024, 2816], P(None, ('hid', 'dm'))
- w_up_grad: float32 [1024, 2816], P(None, ('hid', 'dm'))
- w_down_grad: float32 [2816, 1024], P(('hid', 'dm'))
Inputs may be any that keep to these rules, and one draw needn't show every extreme that they name: `doc_lengths`: each packed row's 8 document lengths sum to 1024, and every row holds one document of the maximum length.
All inputs are finite; a program needn't handle non-finite values.
Results may differ from a plain program's by a relative error of at most 0.017.
Values may be sent and summed in bfloat16 or wider, within the bound.
A program may use at most 192 MiB of HBM per device.

v0:
```python
import jax
import jax.numpy as jnp
from jax import lax
from jax.sharding import PartitionSpec as P

HD = 64
epsilon = 1e-06


def rms_scale(values, gain_vec):
    return (
        values * lax.rsqrt(jnp.mean(values * values, axis=-1, keepdims=True) + epsilon) * gain_vec
    )


def rope_tables(length, head_dim):
    half_dim = head_dim // 2
    places = jnp.arange(length).astype(jnp.float32)
    frequency = 10000.0 ** (-2.0 * jnp.arange(half_dim).astype(jnp.float32) / head_dim)
    angles = places[:, None] * frequency[None, :]
    return (jnp.cos(angles), jnp.sin(angles))


def rotate(values, cosine, sine_part):
    half_dim = values.shape[-1] // 2
    first_half = values[..., :half_dim]
    second_half = values[..., half_dim:]
    return jnp.concatenate(
        [
            first_half * cosine - second_half * sine_part,
            second_half * cosine + first_half * sine_part,
        ],
        axis=-1,
    )


def plain_dot(left_mat, right_mat):
    return jnp.dot(left_mat, right_mat, preferred_element_type=jnp.float32)


def contract_rows(left_mat, right_mat):
    return lax.dot_general(
        left_mat, right_mat, (((0,), (0,)), ((), ())), preferred_element_type=jnp.float32
    )


def contract_cols(left_mat, right_mat):
    return lax.dot_general(
        left_mat, right_mat, (((1,), (1,)), ((), ())), preferred_element_type=jnp.float32
    )


def swiglu(gate_in, up_in):
    return jax.nn.silu(gate_in) * up_in


def allowed_pairs(segment_row):
    places = jnp.arange(segment_row.shape[0])
    return (segment_row[:, None] == segment_row[None, :]) & (places[:, None] >= places[None, :])


def head_forward(head_items):
    query_head, key_head, value_head, segment_row = head_items
    score_scale = query_head.shape[-1] ** (-0.5)
    scores = jnp.where(
        allowed_pairs(segment_row), contract_cols(query_head, key_head) * score_scale, -1e30
    )
    row_max = jnp.max(scores, axis=-1, keepdims=True)
    weights_exp = jnp.exp(scores - row_max)
    row_total = jnp.sum(weights_exp, axis=-1, keepdims=True)
    weights_soft = weights_exp / row_total
    attended = plain_dot(weights_soft.astype(jnp.bfloat16), value_head)
    return (attended, row_max[:, 0] + jnp.log(row_total[:, 0]))


def head_backward(head_items):
    query_head, key_head, value_head, segment_row, grad_head, log_total = head_items
    score_scale = query_head.shape[-1] ** (-0.5)
    allowed = allowed_pairs(segment_row)
    scores = jnp.where(allowed, contract_cols(query_head, key_head) * score_scale, -1e30)
    weights_soft = jnp.where(allowed, jnp.exp(scores - log_total[:, None]), 0.0)
    grad_soft = contract_cols(grad_head, value_head)
    delta_row = jnp.sum(grad_soft * weights_soft, axis=-1, keepdims=True)
    grad_scores = (weights_soft * (grad_soft - delta_row)).astype(jnp.bfloat16)
    grad_query = plain_dot(grad_scores, key_head) * score_scale
    grad_key = contract_rows(grad_scores, query_head) * score_scale
    grad_mixed = contract_rows(weights_soft.astype(jnp.bfloat16), grad_head)
    return (grad_query, grad_key, grad_mixed)


def on_device(
    tokens,
    first_values,
    doc_lengths,
    cotangent,
    attn_gain,
    w_query,
    w_key,
    w_value,
    w_out,
    mlp_gain,
    w_gate,
    w_up,
    w_down,
):
    row_count = doc_lengths.shape[0]
    tok_count, model_width = tokens.shape
    length = tok_count // row_count
    head_count = model_width // HD
    full_query, full_key, full_value, full_out, gain_first, gain_second = (
        lax.all_gather(w_query, ("dp", "hid", "dm"), axis=0, tiled=True),
        lax.all_gather(w_key, ("dp", "hid", "dm"), axis=0, tiled=True),
        lax.all_gather(w_value, ("dp", "hid", "dm"), axis=0, tiled=True),
        lax.all_gather(w_out, ("dp", "hid", "dm"), axis=0, tiled=True),
        lax.all_gather(attn_gain, ("dp", "hid", "dm"), axis=0, tiled=True),
        lax.all_gather(mlp_gain, ("dp", "hid", "dm"), axis=0, tiled=True),
    )
    gain_one = gain_first.astype(jnp.float32)
    gain_two = gain_second.astype(jnp.float32)
    doc_ends = jnp.cumsum(doc_lengths, axis=1)
    places = jnp.arange(length)
    segments = jnp.sum((places[None, :, None] >= doc_ends[:, None, :]).astype(jnp.int32), axis=2)
    head_segments = jnp.repeat(segments, head_count, axis=0)
    cosine, sine_part = rope_tables(length, HD)
    cosine = cosine[:, None, :]
    sine_part = sine_part[:, None, :]

    def to_heads(flat_rows):
        return flat_rows.reshape(row_count, length, head_count, HD)

    def head_major(split_rows):
        return split_rows.transpose(0, 2, 1, 3).reshape(row_count * head_count, length, HD)

    def unheads(stacked):
        return stacked.reshape(row_count, head_count, length, HD).transpose(0, 2, 1, 3)

    inputs = tokens.astype(jnp.float32)
    normed = rms_scale(inputs, gain_one).astype(jnp.bfloat16)
    query_rot = head_major(
        rotate(to_heads(plain_dot(normed, full_query)), cosine, sine_part).astype(jnp.bfloat16)
    )
    key_rot = head_major(
        rotate(to_heads(plain_dot(normed, full_key)), cosine, sine_part).astype(jnp.bfloat16)
    )
    mixed_values = head_major(
        to_heads(
            (0.5 * plain_dot(normed, full_value) + 0.5 * first_values.astype(jnp.float32)).astype(
                jnp.bfloat16
            )
        )
    )
    attended, log_totals = lax.map(head_forward, (query_rot, key_rot, mixed_values, head_segments))
    attn_rows = unheads(attended).reshape(tok_count, model_width).astype(jnp.bfloat16)
    middle = inputs + plain_dot(attn_rows, full_out)
    normed_two = rms_scale(middle, gain_two).astype(jnp.bfloat16)
    gate_full, up_full, down_full = (
        lax.all_gather(w_gate, ("hid", "dm"), axis=1, tiled=True),
        lax.all_gather(w_up, ("hid", "dm"), axis=1, tiled=True),
        lax.all_gather(w_down, ("hid", "dm"), axis=0, tiled=True),
    )
    hidden_f, silu_back = jax.vjp(
        swiglu, plain_dot(normed_two, gate_full), plain_dot(normed_two, up_full)
    )
    hidden = hidden_f.astype(jnp.bfloat16)
    mlp_result = plain_dot(hidden, down_full)
    grad_gate_f, grad_up_f = silu_back(contract_cols(cotangent, down_full))
    grad_gate_act = grad_gate_f.astype(jnp.bfloat16)
    grad_up_act = grad_up_f.astype(jnp.bfloat16)
    grad_normed_two = contract_cols(grad_gate_act, gate_full) + contract_cols(grad_up_act, up_full)
    local_gate = contract_rows(normed_two, grad_gate_act)
    local_up = contract_rows(normed_two, grad_up_act)
    local_down = contract_rows(hidden, cotangent)
    output = (middle + mlp_result).astype(jnp.bfloat16)
    norm_two_value, norm_two_back = jax.vjp(rms_scale, middle, gain_two)
    grad_mid_norm, grad_gain_two = norm_two_back(grad_normed_two)
    grad_middle = cotangent.astype(jnp.float32) + grad_mid_norm
    grad_branch = grad_middle.astype(jnp.bfloat16)
    back_query, back_key, back_value, back_out, back_first = (
        lax.all_gather(w_query, ("dp", "hid", "dm"), axis=0, tiled=True),
        lax.all_gather(w_key, ("dp", "hid", "dm"), axis=0, tiled=True),
        lax.all_gather(w_value, ("dp", "hid", "dm"), axis=0, tiled=True),
        lax.all_gather(w_out, ("dp", "hid", "dm"), axis=0, tiled=True),
        lax.all_gather(attn_gain, ("dp", "hid", "dm"), axis=0, tiled=True),
    )
    back_gain = back_first.astype(jnp.float32)
    out_grad = contract_rows(attn_rows, grad_branch)
    grad_attended = head_major(to_heads(contract_cols(grad_branch, back_out).astype(jnp.bfloat16)))
    grad_query_rot, grad_key_rot, grad_mixed = lax.map(
        head_backward, (query_rot, key_rot, mixed_values, head_segments, grad_attended, log_totals)
    )
    grad_query_rows = (
        rotate(unheads(grad_query_rot), cosine, -sine_part)
        .reshape(tok_count, model_width)
        .astype(jnp.bfloat16)
    )
    grad_key_rows = (
        rotate(unheads(grad_key_rot), cosine, -sine_part)
        .reshape(tok_count, model_width)
        .astype(jnp.bfloat16)
    )
    values_grad = (0.5 * unheads(grad_mixed).reshape(tok_count, model_width)).astype(jnp.bfloat16)
    query_grad = contract_rows(normed, grad_query_rows)
    key_grad = contract_rows(normed, grad_key_rows)
    value_w_grad = contract_rows(normed, values_grad)
    grad_normed = (
        contract_cols(grad_query_rows, back_query)
        + contract_cols(grad_key_rows, back_key)
        + contract_cols(values_grad, back_value)
    )
    norm_one_value, norm_one_back = jax.vjp(rms_scale, inputs, back_gain)
    grad_in_norm, grad_gain_one = norm_one_back(grad_normed)
    tokens_grad = (grad_middle + grad_in_norm).astype(jnp.bfloat16)
    part_gate, part_up, part_down = (
        lax.psum_scatter(
            local_gate.astype(jnp.bfloat16), ("hid", "dm"), scatter_dimension=1, tiled=True
        ).astype(jnp.float32),
        lax.psum_scatter(
            local_up.astype(jnp.bfloat16), ("hid", "dm"), scatter_dimension=1, tiled=True
        ).astype(jnp.float32),
        lax.psum_scatter(
            local_down.astype(jnp.bfloat16), ("hid", "dm"), scatter_dimension=0, tiled=True
        ).astype(jnp.float32),
    )
    gate_grad, up_grad, down_grad = (
        lax.psum(part_gate.astype(jnp.bfloat16), "dp").astype(jnp.float32),
        lax.psum(part_up.astype(jnp.bfloat16), "dp").astype(jnp.float32),
        lax.psum(part_down.astype(jnp.bfloat16), "dp").astype(jnp.float32),
    )
    query_sum, key_sum, value_sum, out_sum, gain_one_sum, gain_two_sum = (
        lax.psum_scatter(query_grad, ("dp", "hid", "dm"), scatter_dimension=0, tiled=True),
        lax.psum_scatter(key_grad, ("dp", "hid", "dm"), scatter_dimension=0, tiled=True),
        lax.psum_scatter(value_w_grad, ("dp", "hid", "dm"), scatter_dimension=0, tiled=True),
        lax.psum_scatter(out_grad, ("dp", "hid", "dm"), scatter_dimension=0, tiled=True),
        lax.psum_scatter(grad_gain_one, ("dp", "hid", "dm"), scatter_dimension=0, tiled=True),
        lax.psum_scatter(grad_gain_two, ("dp", "hid", "dm"), scatter_dimension=0, tiled=True),
    )
    return (
        output,
        tokens_grad,
        values_grad,
        query_sum,
        key_sum,
        value_sum,
        out_sum,
        gain_one_sum,
        gain_two_sum,
        gate_grad,
        up_grad,
        down_grad,
    )


def solution(mesh):
    return jax.shard_map(
        on_device,
        mesh=mesh,
        in_specs=(
            P(("dp", "hid", "dm"), None),
            P(("dp", "hid", "dm"), None),
            P(("dp", "hid", "dm"), None),
            P(("dp", "hid", "dm"), None),
            P(("dp", "hid", "dm")),
            P(("dp", "hid", "dm"), None),
            P(("dp", "hid", "dm"), None),
            P(("dp", "hid", "dm"), None),
            P(("dp", "hid", "dm"), None),
            P(("dp", "hid", "dm")),
            P(None, ("hid", "dm")),
            P(None, ("hid", "dm")),
            P(("hid", "dm"), None),
        ),
        out_specs=(
            P(("dp", "hid", "dm"), None),
            P(("dp", "hid", "dm"), None),
            P(("dp", "hid", "dm"), None),
            P(("dp", "hid", "dm"), None),
            P(("dp", "hid", "dm"), None),
            P(("dp", "hid", "dm"), None),
            P(("dp", "hid", "dm"), None),
            P(("dp", "hid", "dm")),
            P(("dp", "hid", "dm")),
            P(None, ("hid", "dm")),
            P(None, ("hid", "dm")),
            P(("hid", "dm"), None),
        ),
        check_vma=False,
    )
```

profile of v0, /device:TPU:0, one launch (start us, length us, event | category | flops | bytes accessed | tf_op | source)
XLA Modules:
  0.0 1386.8 jit_solution(16985763490271452871)
XLA Ops:
  13.6 2.9 copy.79
  17.5 42.0 %all-reduce.5 = (bf16[1024]{0:T(1024)(128)(2,1)S(1)}, bf16[1024]{0:T(1024)(128)(2,1)S(1)}) all-reduce(bf16[1024]{0:T(1024)(128)(2,1)S(1)} %dynamic-update-slice, bf16[1024]{0:T(1024)(128)(2,1)S(1)} %dynamic-update-slice.1), channel_id=1, replica_groups=mesh['dp'=4,'hid'=2,'dm'=4] {'dp','hid','dm'}, use_global_device_ids=true, to_apply=%add | all-reduce | flops 2048 | bytes 8192
  59.5 4.0 copy.80
  65.0 5.0 all-gather.8.cloned.1.call-done
  70.0 6.1 fusion.74
  76.0 52.0 %all-gather.10.cloned.1.call-done = bf16[1024,1024]{1,0:T(8,128)(2,1)} async-done(((bf16[32,1024]{1,0:T(8,128)(2,1)}), bf16[1024,1024]{1,0:T(8,128)(2,1)}) %all-gather.10.cloned.1.call-update) | async-done | bytes 2097168 | tf_op jit(solution)/shard_map/all_gather | solution.py:112
  128.1 4.3 fusion.72
  136.4 4.8 copy.82
  141.2 4.7 copy.83
  145.9 40.2 %all-gather.12.cloned.1.call-done = bf16[1024,1024]{1,0:T(8,128)(2,1)} async-done(((bf16[32,1024]{1,0:T(8,128)(2,1)}), bf16[1024,1024]{1,0:T(8,128)(2,1)}) %all-gather.12.cloned.1.call-update) | async-done | bytes 2097168 | tf_op jit(solution)/shard_map/all_gather | solution.py:113
  186.1 6.2 multiply_convert_fusion.5
  192.3 5.2 copy.81
  197.5 136.9 %while.28 = (s32[]{:T(128)}, bf16[16,1024,64]{1,2,0:T(8,128)(2,1)}, f32[16,1024]{1,0:T(8,128)S(1)}, s32[16,1024]{1,0:T(8,128)S(1)}, bf16[16,1024,64]{2,1,0:T(8,1...) while((s32[]{:T(128)}, bf16[16,1024,64]{1,2,0:T(8,128)(2,1)}, ...), condition=%wide.region_6.7_spmd.clone, body=%wide.region_3.6_spmd.sunk.clone | while | flops 279968768 | bytes 30468208 | solution.py:152
  202.3 3.7 fusion.151
  210.8 3.8 fusion.151
  219.4 3.8 fusion.151
  227.9 4.0 fusion.151
  236.7 3.8 fusion.151
  245.2 3.7 fusion.151
  253.7 3.7 fusion.151
  262.2 3.7 fusion.151
  270.7 3.7 fusion.151
  279.2 3.7 fusion.151
  287.7 3.7 fusion.151
  296.2 4.1 fusion.151
  305.1 3.7 fusion.151
  313.6 3.8 fusion.151
  322.1 3.7 fusion.151
  330.6 3.8 fusion.151
  334.5 4.8 multiply_reduce_fusion.3
  343.0 11.7 fusion.77
  354.7 12.2 fusion.78
  366.9 10.9 all-gather.20.cloned.1.call-done
  377.8 21.6 %multiply_convert_fusion.1 = (bf16[1024,2816]{1,0:T(8,128)(2,1)}, bf16[1024,2816]{1,0:T(8,128)(2,1)}, bf16[1024,2816]{1,0:T(8,128)(2,1)}) fusion(f32[1024,2816]{1,0:T(8,128)} %fusion.77, f32[1024,2816]{1,0:T(8,128)} %fusion.78, bf16[1024,1024]{1,0:T(8,128)(2,1)S(1)} %copy-done.10, bf16[2816,1024]{1,0:T(8,128)(2,1)} %all-gather.20.cloned.1.call-done), kind=kOutput, calls=%fused_computation.60 | convolution fusion | flops 5951717376 | bytes 48234496 | tf_op jit(solution)/shard_map/dot_general | solution.py:48
  399.4 11.0 convolution_convert_fusion.2
  410.5 11.3 convolution_convert_fusion.1
  421.8 11.3 convolution_convert_fusion
  433.2 3.5 copy.85
  436.8 11.4 fusion.79
  448.2 11.3 multiply_reduce_fusion.1
  463.5 3.2 copy.88
  466.7 2.9 reduce-scatter.16.cloned.1.call-done
  469.6 62.5 %reduce-scatter.18.cloned.1.call-done = bf16[1024,352]{0,1:T(8,128)(2,1)} async-done(((bf16[1024,2816]{0,1:T(8,128)(2,1)}), bf16[1024,352]{0,1:T(8,128)(2,1)}) %reduce-scatter.18.cloned.1.call-update) | async-done | bytes 720912 | tf_op jit(solution)/shard_map/reduce_scatter | solution.py:217
  532.1 62.3 %reduce-scatter.20.cloned.1.call-done = bf16[352,1024]{1,0:T(8,128)(2,1)} async-done(((bf16[2816,1024]{1,0:T(8,128)(2,1)}), bf16[352,1024]{1,0:T(8,128)(2,1)}) %reduce-scatter.20.cloned.1.call-update) | async-done | bytes 720912 | tf_op jit(solution)/shard_map/reduce_scatter | solution.py:220
  594.5 205.6 %while.29 = (s32[]{:T(128)}, f32[16,1024,64]{1,2,0:T(8,128)}, f32[16,1024,64]{1,2,0:T(8,128)}, f32[16,1024,64]{1,2,0:T(8,128)}, s32[16,1024]{1,0:T(8,128)S(1)}, ...) while((s32[]{:T(128)}, f32[16,1024,64]{1,2,0:T(8,128)}, ...), condition=%wide.region_11.12_spmd.clone, body=%wide.region_9.11_spmd.sunk.clone | while | flops 684850176 | bytes 34120812 | solution.py:188
  607.5 2.8 exponential_select_fusion.3
  646.1 2.8 exponential_select_fusion.3
  671.8 2.9 exponential_select_fusion.3
  800.1 5.8 subtract_convert_fusion
  808.3 4.4 fusion.67
  815.5 4.3 fusion.69
  819.9 7.2 fusion.59
  831.5 4.3 fusion.65
  835.9 4.0 copy.96
  839.8 4.7 fusion.81
  846.9 5.1 fusion.53
  852.1 40.4 %all-reduce.4 = (f32[1024]{0:T(1024)S(1)}, f32[1024]{0:T(1024)S(1)}) all-reduce(f32[1024]{0:T(1024)S(1)} %get-tuple-element.227, f32[1024]{0:T(1024)S(1)} %get-tuple-element.225), channel_id=6, replica_groups=mesh['dp'=4,'hid'=2,'dm'=4] {'dp','hid','dm'}, use_global_device_ids=true, to_apply=%region_18.19.clone | all-reduce | flops 2048 | bytes 16384
  893.6 5.9 fusion.56
  899.5 3.9 copy.95
  903.5 10.6 add_convert_fusion
  922.7 32.8 %reduce-scatter.10.cloned.1.call-done = f32[32,1024]{1,0:T(8,128)} async-done(((f32[1024,1024]{1,0:T(8,128)}), f32[32,1024]{1,0:T(8,128)}) %reduce-scatter.10.cloned.1.call-update) | async-done | bytes 131088 | tf_op jit(solution)/shard_map/reduce_scatter | solution.py:231
  955.6 141.6 %reduce-scatter.8.cloned.1.call-done = f32[32,1024]{1,0:T(8,128)} async-done(((f32[1024,1024]{1,0:T(8,128)}), f32[32,1024]{1,0:T(8,128)}) %reduce-scatter.8.cloned.1.call-update) | async-done | bytes 131088 | tf_op jit(solution)/shard_map/reduce_scatter | solution.py:230
  1097.2 141.5 %reduce-scatter.14.cloned.1.call-done = f32[32,1024]{1,0:T(8,128)} async-done(((f32[1024,1024]{1,0:T(8,128)}), f32[32,1024]{1,0:T(8,128)}) %reduce-scatter.14.cloned.1.call-update) | async-done | bytes 131088 | tf_op jit(solution)/shard_map/reduce_scatter | solution.py:233
  1238.6 141.2 %reduce-scatter.12.cloned.1.call-done = f32[32,1024]{1,0:T(8,128)} async-done(((f32[1024,1024]{1,0:T(8,128)}), f32[32,1024]{1,0:T(8,128)}) %reduce-scatter.12.cloned.1.call-update) | async-done | bytes 131088 | tf_op jit(solution)/shard_map/reduce_scatter | solution.py:232
  (366 shorter events, 314.2 us)
Async XLA Ops:
  7.2 62.8 %all-gather.8.cloned.1.call-start = ((), (), s32[]{:S(2)}) async-start(), calls=%async_computation.7 | async-start | bytes 2162688 | tf_op jit(solution)/shard_map/all_gather | solution.py:111
  7.9 120.1 %all-gather.10.cloned.1.call-start = ((), (), s32[]{:S(2)}) async-start(), calls=%async_computation.8 | async-start | bytes 2162688 | tf_op jit(solution)/shard_map/all_gather | solution.py:112
  8.7 177.4 %all-gather.12.cloned.1.call-start = ((), (), s32[]{:S(2)}) async-start(), calls=%async_computation.9 | async-start | bytes 2162688 | tf_op jit(solution)/shard_map/all_gather | solution.py:113
  9.4 325.1 %all-gather.14.cloned.1.call-start = ((), (), s32[]{:S(2)}) async-start(), calls=%async_computation.10 | async-start | bytes 2162688 | tf_op jit(solution)/shard_map/all_gather | solution.py:114
  10.0 331.7 %all-gather.16.cloned.1.call-start = ((), (), s32[]{:S(2)}) async-start(), calls=%async_computation.11 | async-start | bytes 6488064 | tf_op jit(solution)/shard_map/all_gather | solution.py:157
  10.6 344.1 %all-gather.18.cloned.1.call-start = ((), (), s32[]{:S(2)}) async-start(), calls=%async_computation.12 | async-start | bytes 6488064 | tf_op jit(solution)/shard_map/all_gather | solution.py:158
  11.1 366.7 %all-gather.20.cloned.1.call-start = ((), (), s32[]{:S(2)}) async-start(), calls=%async_computation.13 | async-start | bytes 6488064 | tf_op jit(solution)/shard_map/all_gather | solution.py:159
  11.9 457.7 %reduce-scatter.16.cloned.1.call-start = ((), (), s32[]{:S(2)}) async-start(), calls=%async_computation.18 | async-start | bytes 6488064 | tf_op jit(solution)/shard_map/reduce_scatter | solution.py:214
  12.0 5.0 copy-start.27
  12.0 5.3 copy-start.28
  16.4 318.1 %copy-start.1 = (bf16[1024,1024]{0,1:T(8,128)(2,1)}, bf16[1024,1024]{0,1:T(8,128)(2,1)S(1)}, u32[]{:S(2)}) copy-start(bf16[1024,1024]{0,1:T(8,128)(2,1)S(1)} %copy.79) | copy-start | bytes 6291460
  16.4 47.0 %copy-start.29 = (s32[1,8]{1,0:T(1,128)S(1)}, s32[1,8]{1,0:T(1,128)}, u32[]{:S(2)}) copy-start(s32[1,8]{1,0:T(1,128)} %param.19) | copy-start | bytes 100
  16.9 46.8 %copy-start.23 = (f32[1024]{0:T(1024)}, f32[1024]{0:T(1024)S(1)}, u32[]{:S(2)}) copy-start(f32[1024]{0:T(1024)S(1)} %fusion.57) | copy-start | bytes 12292
  16.9 169.1 %copy-start.21 = (f32[1024]{0:T(1024)}, f32[1024]{0:T(1024)S(1)}, u32[]{:S(2)}) copy-start(f32[1024]{0:T(1024)S(1)} %fusion.63) | copy-start | bytes 12292
  59.5 126.6 %copy-start.19 = (f32[1024]{0:T(1024)}, f32[1024]{0:T(1024)S(1)}, u32[]{:S(2)}) copy-start(f32[1024]{0:T(1024)S(1)} %convert_element_type.216) | copy-start | bytes 12292
  65.0 67.5 %copy-start.15 = (f32[1024,32]{0,1:T(8,128)}, f32[1024,32]{0,1:T(8,128)S(1)}, u32[]{:S(2)}) copy-start(f32[1024,32]{0,1:T(8,128)S(1)} %get-tuple-element.291) | copy-start | bytes 393220
  128.1 4.4 copy-start.9
  199.6 2.0 copy-start
  208.1 2.0 copy-start
  216.6 2.0 copy-start
  225.2 2.0 copy-start
  233.9 2.0 copy-start
  242.5 2.0 copy-start
  251.0 2.0 copy-start
  259.5 2.0 copy-start
  268.0 2.0 copy-start
  276.5 2.0 copy-start
  285.0 2.0 copy-start
  293.5 2.0 copy-start
  302.4 2.0 copy-start
  310.9 2.0 copy-start
  319.4 2.0 copy-start
  327.9 2.0 copy-start
  339.3 2.0 copy-start.6
  341.7 1.3 copy-start.14
  354.7 23.1 %copy-start.10 = (bf16[1024,1024]{1,0:T(8,128)(2,1)S(1)}, bf16[1024,1024]{1,0:T(8,128)(2,1)}, u32[]{:S(2)}) copy-start(bf16[1024,1024]{1,0:T(8,128)(2,1)} %param.20) | copy-start | bytes 6291460
  410.4 121.6 %reduce-scatter.18.cloned.1.call-start = ((), (), s32[]{:S(2)}) async-start(), calls=%async_computation.19 | async-start | bytes 6488064 | tf_op jit(solution)/shard_map/reduce_scatter | solution.py:217
  421.8 172.6 %reduce-scatter.20.cloned.1.call-start = ((), (), s32[]{:S(2)}) async-start(), calls=%async_computation.20 | async-start | bytes 6488064 | tf_op jit(solution)/shard_map/reduce_scatter | solution.py:220
  433.2 483.5 %all-reduce.9.cloned.1.call-start = ((), (), s32[]{:S(2)}) async-start(), calls=%async_computation.21 | async-start | bytes 4325376 | tf_op jit(solution)/shard_map/psum | solution.py:225
  436.8 11.4 copy-start.7
  459.6 1.6 copy-start.26
  461.2 2.3 copy-start.5
  594.4 361.2 %reduce-scatter.10.cloned.1.call-start = ((), (), s32[]{:S(2)}) async-start(), calls=%async_computation.15 | async-start | bytes 4325376 | tf_op jit(solution)/shard_map/reduce_scatter | solution.py:231
  594.4 205.7 %copy-start.16 = (f32[1024,32]{0,1:T(8,128)S(1)}, f32[1024,32]{0,1:T(8,128)}, u32[]{:S(2)}) copy-start(f32[1024,32]{0,1:T(8,128)} %copy-done.15) | copy-start | bytes 393220
  594.5 205.6 %copy-start.18 = (f32[1024,32]{0,1:T(8,128)S(1)}, f32[1024,32]{0,1:T(8,128)}, u32[]{:S(2)}) copy-start(f32[1024,32]{0,1:T(8,128)} %get-tuple-element.289) | copy-start | bytes 393220
  805.9 2.3 copy-start.2
  805.9 2.3 copy-start.20
  805.9 2.3 copy-start.22
  806.2 1.4 copy-start.11
  812.7 284.5 %reduce-scatter.8.cloned.1.call-start = ((), (), s32[]{:S(2)}) async-start(), calls=%async_computation.14 | async-start | bytes 4325376 | tf_op jit(solution)/shard_map/reduce_scatter | solution.py:230
  814.2 1.3 copy-start.12
  819.9 418.8 %reduce-scatter.14.cloned.1.call-start = ((), (), s32[]{:S(2)}) async-start(), calls=%async_computation.17 | async-start | bytes 4325376 | tf_op jit(solution)/shard_map/reduce_scatter | solution.py:233
  827.1 552.7 %reduce-scatter.12.cloned.1.call-start = ((), (), s32[]{:S(2)}) async-start(), calls=%async_computation.16 | async-start | bytes 4325376 | tf_op jit(solution)/shard_map/reduce_scatter | solution.py:232
  830.2 1.3 copy-start.3
  839.8 4.7 copy-start.13
  839.8 4.7 copy-start.25
  844.6 2.4 copy-start.4
  844.6 2.4 copy-start.8
  846.9 46.6 %copy-start.24 = (f32[1024]{0:T(1024)S(1)}, f32[1024]{0:T(1024)}, u32[]{:S(2)}) copy-start(f32[1024]{0:T(1024)} %copy-done.23) | copy-start | bytes 12292
  916.7 4.8 copy-start.17
Sparse Core Ops, SparseCore 0:
  10.8 59.0 all-gather.7
  72.8 55.1 all-gather.9
  130.9 55.0 all-gather.11
  188.8 55.1 all-gather.13
  245.7 42.0 all-gather.15
  289.5 43.1 all-gather.17
  334.6 43.1 all-gather.19
  410.5 58.9 reduce-scatter.15
  473.0 58.9 reduce-scatter.17
  535.3 58.9 reduce-scatter.19
  597.0 88.2 all-reduce.8
  812.8 142.6 reduce-scatter.9
  958.4 138.6 reduce-scatter.7
  1099.9 138.7 reduce-scatter.13
  1241.3 138.4 reduce-scatter.11
where the time goes:
time: 1400 us; the launch traced here: 1390 us
  waiting for transfers between devices  697 us (50%)
  matrix products  448 us (32%)
  blocking collectives  82.4 us (6%)
  local copies, waits for them, and re-layouts  82.3 us (6%)
  other arithmetic  59.5 us (4%)
  between operations  14.8 us (1%)
    dot_general x55, matrix products, contract_cols(): lax.dot_general(left_mat, right_mat, (((1,), (1,)), ((), ())), preferred_...  165 us
    dot_general x39, matrix products, plain_dot(): return jnp.dot(left_mat, right_mat, preferred_element_type=jnp.float32)  152 us
    reduce_scatter x1, waiting for transfers between devices, on_device(): lax.psum_scatter(query_grad, ('dp', 'hid', 'dm'), scatter_dimension=0, ti...  142 us
    reduce_scatter x1, waiting for transfers between devices, on_device(): lax.psum_scatter(out_grad, ('dp', 'hid', 'dm'), scatter_dimension=0, tile...  141 us
    reduce_scatter x1, waiting for transfers between devices, on_device(): lax.psum_scatter(value_w_grad, ('dp', 'hid', 'dm'), scatter_dimension=0,...  141 us
    dot_general x39, matrix products, contract_rows(): lax.dot_general(left_mat, right_mat, (((0,), (0,)), ((), ())), preferred_...  132 us
    unnamed x2, blocking collectives  82.4 us
    reduce_scatter x1, waiting for transfers between devices, on_device(): lax.psum_scatter(local_up.astype(jnp.bfloat16), ('hid', 'dm'), scatter_di...  62.5 us
  transfers between devices with their start and end apart: 15, of which 11 were waited for; matrix products, arithmetic and copies ran while one was open for 37% of the time, Pallas kernels for 0%

commit v1 on v0

--- a/solution.py
+++ b/solution.py
@@ -5,6 +5,18 @@
 
 HD = 64
 epsilon = 1e-06
+
+
+def collect(x, axis, dim):
+    ways, here, step = (lax.axis_size(axis), lax.axis_index(axis), x.shape[dim])
+    line, have = (x, 1)
+    while have < ways:
+        line = jnp.concatenate(
+            [line, lax.ppermute(line, axis, [(d, (d - have) % ways) for d in range(ways)])],
+            axis=dim,
+        )
+        have = 2 * have
+    return jnp.roll(line, here * step, axis=dim)
 
 
 def rms_scale(values, gain_vec):
@@ -110,7 +122,7 @@
     full_query, full_key, full_value, full_out, gain_first, gain_second = (
         lax.all_gather(w_query, ("dp", "hid", "dm"), axis=0, tiled=True),
         lax.all_gather(w_key, ("dp", "hid", "dm"), axis=0, tiled=True),
-        lax.all_gather(w_value, ("dp", "hid", "dm"), axis=0, tiled=True),
+        collect(w_value, ("dp", "hid", "dm"), 0),
         lax.all_gather(w_out, ("dp", "hid", "dm"), axis=0, tiled=True),
         lax.all_gather(attn_gain, ("dp", "hid", "dm"), axis=0, tiled=True),
         lax.all_gather(mlp_gain, ("dp", "hid", "dm"), axis=0, tiled=True),

time: 1400 us -> 1320 us (0.943)
  waiting for transfers between devices: 697 us -> 554 us
  local copies, waits for them, and re-layouts: 82.3 us -> 127 us
    reduce_scatter x1, waiting for transfers between devices: 141 us -> 0.01 us  [on_device(): lax.psum_scatter(out_grad, ('dp', 'hid', 'dm'), scatter_dimension=0, tile...]
    reduce_scatter x1, waiting for transfers between devices: 2.9 us -> 62.5 us  [on_device(): lax.psum_scatter(local_gate.astype(jnp.bfloat16), ('hid', 'dm'), scatter_...]
    ppermute x0 -> x5, waiting for transfers between devices: none -> 58.5 us  [collect(): lax.ppermute(line, axis, [(d, (d - have) % ways) for d in range(ways)])]
    all_gather x1, waiting for transfers between devices: 52 us -> 8.29 us  [on_device(): lax.all_gather(w_key, ('dp', 'hid', 'dm'), axis=0, tiled=True)]
    reduce_scatter x1, waiting for transfers between devices: 62.5 us -> 21.1 us  [on_device(): lax.psum_scatter(local_up.astype(jnp.bfloat16), ('hid', 'dm'), scatter_di...]
    all_gather x1, waiting for transfers between devices: 40.2 us -> 0.01 us  [on_device(): lax.all_gather(w_value, ('dp', 'hid', 'dm'), axis=0, tiled=True)]
    reduce_scatter x1, waiting for transfers between devices: 32.8 us -> 54.9 us  [on_device(): lax.psum_scatter(key_grad, ('dp', 'hid', 'dm'), scatter_dimension=0, tile...]
    dynamic_update_slice x16, local copies, waits for them, and re-layouts: 1.72 us -> 22.4 us  [on_device(): lax.map(head_forward, (query_rot, key_rot, mixed_values, head_segments))]
  transfers between devices with their start and end apart: 15 -> 20, of which waited for: 11 -> 11; matrix products, arithmetic and copies ran while one was open for 37% -> 44% of each run, Pallas kernels for 0% -> 0%
where the time goes in v1:
time: 1320 us; the launch traced here: 1310 us
  waiting for transfers between devices  554 us (42%)
  matrix products  455 us (34%)
  local copies, waits for them, and re-layouts  127 us (10%)
  blocking collectives  80.4 us (6%)
  other arithmetic  62.9 us (5%)
  between operations  15 us (1%)
  starting transfers between devices  13.3 us (1%)
    dot_general x55, matrix products, contract_cols(): lax.dot_general(left_mat, right_mat, (((1,), (1,)), ((), ())), preferred_...  174 us
    dot_general x39, matrix products, plain_dot(): return jnp.dot(left_mat, right_mat, preferred_element_type=jnp.float32)  149 us
    reduce_scatter x1, waiting for transfers between devices, on_device(): lax.psum_scatter(query_grad, ('dp', 'hid', 'dm'), scatter_dimension=0, ti...  141 us
    reduce_scatter x1, waiting for transfers between devices, on_device(): lax.psum_scatter(value_w_grad, ('dp', 'hid', 'dm'), scatter_dimension=0,...  141 us
    dot_general x39, matrix products, contract_rows(): lax.dot_general(left_mat, right_mat, (((0,), (0,)), ((), ())), preferred_...  132 us
    unnamed x2, blocking collectives  80.4 us
    reduce_scatter x1, waiting for transfers between devices, on_device(): lax.psum_scatter(local_down.astype(jnp.bfloat16), ('hid', 'dm'), scatter_...  62.5 us
    reduce_scatter x1, waiting for transfers between devices, on_device(): lax.psum_scatter(local_gate.astype(jnp.bfloat16), ('hid', 'dm'), scatter_...  62.5 us
  transfers between devices with their start and end apart: 20, of which 11 were waited for; matrix products, arithmetic and copies ran while one was open for 44% of the time, Pallas kernels for 0%

profile of v1, /device:TPU:0, one launch (start us, length us, event | category | flops | bytes accessed | tf_op | source)
XLA Modules:
  0.0 1308.9 jit_solution(17823221114631650567)
XLA Ops:
  10.6 6.5 collective-permute-start
  20.8 4.6 collective-permute-done.1
  26.7 7.5 collective-permute-done.2
  38.0 2.9 copy.79
  41.4 40.5 %all-reduce.5 = (bf16[1024]{0:T(1024)(128)(2,1)S(1)}, bf16[1024]{0:T(1024)(128)(2,1)S(1)}) all-reduce(bf16[1024]{0:T(1024)(128)(2,1)S(1)} %dynamic-update-slice, bf16[1024]{0:T(1024)(128)(2,1)S(1)} %dynamic-update-slice.1), channel_id=1, replica_groups=mesh['dp'=4,'hid'=2,'dm'=4] {'dp','hid','dm'}, use_global_device_ids=true, to_apply=%add | all-reduce | flops 2048 | bytes 8192
  81.9 3.9 copy.80
  86.3 3.1 collective-permute-start.4
  93.3 44.2 %collective-permute-done.4 = bf16[512,1024]{1,0:T(8,128)(2,1)S(1)} collective-permute-done((bf16[512,1024]{1,0:T(8,128)(2,1)S(1)}, bf16[512,1024]{1,0:T(8,128)(2,1)S(1)}, u32[]{:S(2)}, u32[]{:S(2)}) %collective-permute-start.4) | collective-permute-done | bytes 1048608 | tf_op jit(solution)/shard_map/ppermute | solution.py:15
  137.8 4.2 multiply_convert_fusion.5
  142.0 4.9 copy.81
  146.9 6.0 fusion.79
  153.0 8.3 all-gather.10.cloned.1.call-done
  161.3 4.3 fusion.77
  169.6 4.8 copy.82
  174.3 4.8 copy.83
  179.1 157.1 %while.28 = (s32[]{:T(128)}, bf16[16,1024,64]{1,2,0:T(8,128)(2,1)}, f32[16,1024]{1,0:T(8,128)}, s32[16,1024]{1,0:T(8,128)S(1)}, bf16[16,1024,64]{2,1,0:T(8,128)(...) while((s32[]{:T(128)}, bf16[16,1024,64]{1,2,0:T(8,128)(2,1)}, ...), condition=%wide.region_6.7_spmd.clone, body=%wide.region_3.6_spmd.sunk.clone | while | flops 279968768 | bytes 30468208 | solution.py:164
  185.1 3.7 fusion.155
  194.9 3.8 fusion.155
  204.6 3.7 fusion.155
  214.4 3.8 fusion.155
  224.1 3.8 fusion.155
  234.0 3.7 fusion.155
  243.8 3.9 fusion.155
  253.7 3.8 fusion.155
  263.5 3.7 fusion.155
  273.2 3.8 fusion.155
  283.1 3.7 fusion.155
  292.8 3.8 fusion.155
  302.6 3.8 fusion.155
  312.4 3.7 fusion.155
  322.2 3.7 fusion.155
  331.9 4.1 fusion.155
  336.2 4.8 multiply_reduce_fusion.3
  344.7 11.6 fusion.82
  356.3 12.0 fusion.83
  368.4 21.9 %multiply_convert_fusion.1 = (bf16[1024,2816]{1,0:T(8,128)(2,1)}, bf16[1024,2816]{1,0:T(8,128)(2,1)}, bf16[1024,2816]{1,0:T(8,128)(2,1)}) fusion(f32[1024,2816]{1,0:T(8,128)} %fusion.82, f32[1024,2816]{1,0:T(8,128)} %fusion.83, bf16[1024,1024]{1,0:T(8,128)(2,1)S(1)} %copy-done.9, bf16[2816,1024]{1,0:T(8,128)(2,1)} %all-gather.18.cloned.1.call-done), kind=kOutput, calls=%fused_computation.60 | convolution fusion | flops 5951717376 | bytes 48234496 | tf_op jit(solution)/shard_map/dot_general | solution.py:60
  390.2 11.1 convolution_convert_fusion.1
  401.4 11.0 convolution_convert_fusion.2
  412.5 11.6 convolution_convert_fusion
  424.8 2.9 copy.85
  427.7 11.2 fusion.84
  438.9 21.1 %reduce-scatter.18.cloned.1.call-done = bf16[1024,352]{0,1:T(8,128)(2,1)} async-done(((bf16[1024,2816]{0,1:T(8,128)(2,1)}), bf16[1024,352]{0,1:T(8,128)(2,1)}) %reduce-scatter.18.cloned.1.call-update) | async-done | bytes 720912 | tf_op jit(solution)/shard_map/reduce_scatter | solution.py:229
  460.0 62.5 %reduce-scatter.16.cloned.1.call-done = bf16[1024,352]{0,1:T(8,128)(2,1)} async-done(((bf16[1024,2816]{0,1:T(8,128)(2,1)}), bf16[1024,352]{0,1:T(8,128)(2,1)}) %reduce-scatter.16.cloned.1.call-update) | async-done | bytes 720912 | tf_op jit(solution)/shard_map/reduce_scatter | solution.py:226
  522.5 62.5 %reduce-scatter.20.cloned.1.call-done = bf16[352,1024]{1,0:T(8,128)(2,1)} async-done(((bf16[2816,1024]{1,0:T(8,128)(2,1)}), bf16[352,1024]{1,0:T(8,128)(2,1)}) %reduce-scatter.20.cloned.1.call-update) | async-done | bytes 720912 | tf_op jit(solution)/shard_map/reduce_scatter | solution.py:232
  585.1 12.7 multiply_reduce_fusion.1
  601.7 3.2 copy.88
  604.9 7.2 fusion.63
  612.2 229.2 %while.29 = (s32[]{:T(128)}, f32[16,1024,64]{1,2,0:T(8,128)}, f32[16,1024,64]{1,2,0:T(8,128)}, f32[16,1024,64]{1,2,0:T(8,128)}, s32[16,1024]{1,0:T(8,128)}, /*in...) while((s32[]{:T(128)}, f32[16,1024,64]{1,2,0:T(8,128)}, ...), condition=%wide.region_11.12_spmd.clone, body=%wide.region_9.11_spmd.sunk.clone | while | flops 684850176 | bytes 34120812 | solution.py:200
  628.2 2.9 exponential_select_fusion.3
  841.4 5.9 subtract_convert_fusion
  849.6 4.3 fusion.72
  856.8 4.4 fusion.74
  865.4 4.4 fusion.70
  869.8 4.2 copy.96
  874.0 6.7 fusion.86
  880.7 4.3 fusion.85
  885.0 9.6 fusion.53
  894.5 39.9 %all-reduce.4 = (f32[1024]{0:T(1024)S(1)}, f32[1024]{0:T(1024)S(1)}) all-reduce(f32[1024]{0:T(1024)S(1)} %get-tuple-element.227, f32[1024]{0:T(1024)S(1)} %get-tuple-element.225), channel_id=6, replica_groups=mesh['dp'=4,'hid'=2,'dm'=4] {'dp','hid','dm'}, use_global_device_ids=true, to_apply=%region_18.19.clone | all-reduce | flops 2048 | bytes 16384
  935.6 5.9 fusion.56
  941.5 3.9 copy.95
  945.5 10.6 add_convert_fusion
  964.7 54.9 %reduce-scatter.10.cloned.1.call-done = f32[32,1024]{1,0:T(8,128)} async-done(((f32[1024,1024]{1,0:T(8,128)}), f32[32,1024]{1,0:T(8,128)}) %reduce-scatter.10.cloned.1.call-update) | async-done | bytes 131088 | tf_op jit(solution)/shard_map/reduce_scatter | solution.py:243
  1019.5 141.2 %reduce-scatter.8.cloned.1.call-done = f32[32,1024]{1,0:T(8,128)} async-done(((f32[1024,1024]{1,0:T(8,128)}), f32[32,1024]{1,0:T(8,128)}) %reduce-scatter.8.cloned.1.call-update) | async-done | bytes 131088 | tf_op jit(solution)/shard_map/reduce_scatter | solution.py:242
  1160.7 141.2 %reduce-scatter.12.cloned.1.call-done = f32[32,1024]{1,0:T(8,128)} async-done(((f32[1024,1024]{1,0:T(8,128)}), f32[32,1024]{1,0:T(8,128)}) %reduce-scatter.12.cloned.1.call-update) | async-done | bytes 131088 | tf_op jit(solution)/shard_map/reduce_scatter | solution.py:244
  (393 shorter events, 370.2 us)
Async XLA Ops:
  7.2 139.8 %all-gather.8.cloned.1.call-start = ((), (), s32[]{:S(2)}) async-start(), calls=%async_computation.7 | async-start | bytes 2162688 | tf_op jit(solution)/shard_map/all_gather | solution.py:123
  7.9 33.0 %copy-start.28 = (bf16[32]{0:T(256)(128)(2,1)S(1)}, bf16[32]{0:T(256)(128)(2,1)}, u32[]{:S(2)}) copy-start(bf16[32]{0:T(256)(128)(2,1)} %param.21) | copy-start | bytes 196
  7.9 33.2 %copy-start.29 = (bf16[32]{0:T(256)(128)(2,1)S(1)}, bf16[32]{0:T(256)(128)(2,1)}, u32[]{:S(2)}) copy-start(bf16[32]{0:T(256)(128)(2,1)} %param.26) | copy-start | bytes 196
  7.9 153.3 %all-gather.10.cloned.1.call-start = ((), (), s32[]{:S(2)}) async-start(), calls=%async_computation.8 | async-start | bytes 2162688 | tf_op jit(solution)/shard_map/all_gather | solution.py:124
  8.7 327.5 %all-gather.12.cloned.1.call-start = ((), (), s32[]{:S(2)}) async-start(), calls=%async_computation.9 | async-start | bytes 2162688 | tf_op jit(solution)/shard_map/all_gather | solution.py:126
  9.4 334.0 %all-gather.14.cloned.1.call-start = ((), (), s32[]{:S(2)}) async-start(), calls=%async_computation.10 | async-start | bytes 6488064 | tf_op jit(solution)/shard_map/all_gather | solution.py:169
  10.0 346.4 %all-gather.16.cloned.1.call-start = ((), (), s32[]{:S(2)}) async-start(), calls=%async_computation.11 | async-start | bytes 6488064 | tf_op jit(solution)/shard_map/all_gather | solution.py:170
  10.6 357.8 %all-gather.18.cloned.1.call-start = ((), (), s32[]{:S(2)}) async-start(), calls=%async_computation.12 | async-start | bytes 6488064 | tf_op jit(solution)/shard_map/all_gather | solution.py:171
  10.6 8.7 collective-permute-start
  20.2 5.3 collective-permute-start.1
  26.3 7.9 collective-permute-start.2
  26.6 433.4 %reduce-scatter.18.cloned.1.call-start = ((), (), s32[]{:S(2)}) async-start(), calls=%async_computation.19 | async-start | bytes 6488064 | tf_op jit(solution)/shard_map/reduce_scatter | solution.py:229
  35.8 50.3 %collective-permute-start.3 = (bf16[256,1024]{1,0:T(8,128)(2,1)}, bf16[256,1024]{1,0:T(8,128)(2,1)S(1)}, u32[]{:S(2)}, u32[]{:S(2)}) collective-permute-start(bf16[256,1024]{1,0:T(8,128)(2,1)} %pad_maximum_fusion.2), channel_id=1, source_target_pairs={{0,24},{1,25},{2,26},{3,27},{4,28},{5,29},{6,30},{7,31},{8,0},{9,1... | collective-permute-start | bytes 1572872 | tf_op jit(solution)/shard_map/ppermute | solution.py:15
  37.9 47.9 %copy-start.30 = (s32[1,8]{1,0:T(1,128)S(1)}, s32[1,8]{1,0:T(1,128)}, u32[]{:S(2)}) copy-start(s32[1,8]{1,0:T(1,128)} %param.19) | copy-start | bytes 100
  37.9 48.1 %copy-start.8 = (bf16[32,1024]{1,0:T(8,128)(2,1)S(1)}, bf16[32,1024]{1,0:T(8,128)(2,1)}, u32[]{:S(2)}) copy-start(bf16[32,1024]{1,0:T(8,128)(2,1)} %param.24) | copy-start | bytes 196612
  40.9 295.4 %copy-start.1 = (bf16[1024,1024]{0,1:T(8,128)(2,1)}, bf16[1024,1024]{0,1:T(8,128)(2,1)S(1)}, u32[]{:S(2)}) copy-start(bf16[1024,1024]{0,1:T(8,128)(2,1)S(1)} %copy.79) | copy-start | bytes 6291460
  81.9 79.4 %copy-start.20 = (f32[1024]{0:T(1024)}, f32[1024]{0:T(1024)S(1)}, u32[]{:S(2)}) copy-start(f32[1024]{0:T(1024)S(1)} %convert_element_type.216) | copy-start | bytes 12292
  86.3 51.3 %collective-permute-start.4 = (bf16[512,1024]{1,0:T(8,128)(2,1)S(1)}, bf16[512,1024]{1,0:T(8,128)(2,1)S(1)}, u32[]{:S(2)}, u32[]{:S(2)}) collective-permute-start(bf16[512,1024]{1,0:T(8,128)(2,1)S(1)} %get-tuple-element.285), channel_id=1, source_target_pairs={{0,16},{1,17},{2,18},{3,19},{4,20},{5,21},{6,22},{7,23},{8,24},{9,... | collective-permute-start | bytes 3145736 | tf_op jit(solution)/shard_map/ppermute | solution.py:15
  91.1 46.8 %copy-start.10 = (bf16[1024,1024]{0,1:T(8,128)(2,1)S(1)}, bf16[1024,1024]{0,1:T(8,128)(2,1)}, u32[]{:S(2)}) copy-start(bf16[1024,1024]{0,1:T(8,128)(2,1)} %copy.80) | copy-start | bytes 6291460
  92.1 69.1 %copy-start.22 = (f32[1024]{0:T(1024)}, f32[1024]{0:T(1024)S(1)}, u32[]{:S(2)}) copy-start(f32[1024]{0:T(1024)S(1)} %fusion.67) | copy-start | bytes 12292
  93.3 72.3 %copy-start.15 = (f32[1024,32]{0,1:T(8,128)}, f32[1024,32]{0,1:T(8,128)S(1)}, u32[]{:S(2)}) copy-start(f32[1024,32]{0,1:T(8,128)S(1)} %get-tuple-element.301) | copy-start | bytes 393220
  161.3 4.4 copy-start.7
  181.2 1.9 copy-start
  190.9 1.9 copy-start
  200.7 1.9 copy-start
  210.4 1.9 copy-start
  220.2 1.9 copy-start
  230.1 1.9 copy-start
  239.8 1.9 copy-start
  249.7 1.9 copy-start
  259.5 1.9 copy-start
  269.3 1.9 copy-start
  279.1 1.9 copy-start
  288.8 1.9 copy-start
  298.6 1.9 copy-start
  308.4 1.9 copy-start
  318.2 1.9 copy-start
  327.9 1.9 copy-start
  336.2 4.9 copy-start.19
  341.1 1.9 copy-start.5
  343.4 1.3 copy-start.14
  356.3 12.0 copy-start.9
  401.3 121.2 %reduce-scatter.16.cloned.1.call-start = ((), (), s32[]{:S(2)}) async-start(), calls=%async_computation.18 | async-start | bytes 6488064 | tf_op jit(solution)/shard_map/reduce_scatter | solution.py:226
  412.4 172.6 %reduce-scatter.20.cloned.1.call-start = ((), (), s32[]{:S(2)}) async-start(), calls=%async_computation.20 | async-start | bytes 6488064 | tf_op jit(solution)/shard_map/reduce_scatter | solution.py:232
  424.1 460.8 %all-gather.20.cloned.1.call-start = ((), (), s32[]{:S(2)}) async-start(), calls=%async_computation.13 | async-start | bytes 2162688 | tf_op jit(solution)/shard_map/all_gather | solution.py:193
  424.7 533.8 %all-reduce.9.cloned.1.call-start = ((), (), s32[]{:S(2)}) async-start(), calls=%async_computation.21 | async-start | bytes 4325376 | tf_op jit(solution)/shard_map/psum | solution.py:237
  585.0 379.7 %reduce-scatter.14.cloned.1.call-start = ((), (), s32[]{:S(2)}) async-start(), calls=%async_computation.17 | async-start | bytes 4325376 | tf_op jit(solution)/shard_map/reduce_scatter | solution.py:245
  585.0 12.7 copy-start.6
  597.8 1.6 copy-start.27
  599.4 2.3 copy-start.4
  612.1 407.4 %reduce-scatter.10.cloned.1.call-start = ((), (), s32[]{:S(2)}) async-start(), calls=%async_computation.15 | async-start | bytes 4325376 | tf_op jit(solution)/shard_map/reduce_scatter | solution.py:243
  612.2 229.3 %copy-start.16 = (f32[1024,32]{0,1:T(8,128)S(1)}, f32[1024,32]{0,1:T(8,128)}, u32[]{:S(2)}) copy-start(f32[1024,32]{0,1:T(8,128)} %copy-done.15) | copy-start | bytes 393220
  612.2 229.2 %copy-start.18 = (f32[1024,32]{0,1:T(8,128)S(1)}, f32[1024,32]{0,1:T(8,128)}, u32[]{:S(2)}) copy-start(f32[1024,32]{0,1:T(8,128)} %get-tuple-element.299) | copy-start | bytes 393220
  847.3 2.3 copy-start.2
  847.3 2.3 copy-start.21
  847.3 2.3 copy-start.23
  847.6 1.4 copy-start.11
  854.0 306.8 %reduce-scatter.8.cloned.1.call-start = ((), (), s32[]{:S(2)}) async-start(), calls=%async_computation.14 | async-start | bytes 4325376 | tf_op jit(solution)/shard_map/reduce_scatter | solution.py:242
  855.5 1.3 copy-start.12
  861.2 440.7 %reduce-scatter.12.cloned.1.call-start = ((), (), s32[]{:S(2)}) async-start(), calls=%async_computation.16 | async-start | bytes 4325376 | tf_op jit(solution)/shard_map/reduce_scatter | solution.py:244
  874.0 6.7 copy-start.13
  874.0 6.7 copy-start.26
  885.0 50.6 %copy-start.25 = (f32[1024]{0:T(1024)S(1)}, f32[1024]{0:T(1024)}, u32[]{:S(2)}) copy-start(f32[1024]{0:T(1024)} %copy-done.24) | copy-start | bytes 12292
  958.6 4.8 copy-start.17
  (2 other events, 1.9 us)
Sparse Core Ops, SparseCore 0:
  10.8 66.5 all-gather.7
  80.3 80.9 all-gather.9
  164.1 55.0 all-gather.11
  221.0 42.0 all-gather.13
  264.8 43.1 all-gather.15
  309.8 43.1 all-gather.17
  401.4 58.5 reduce-scatter.17
  463.5 58.9 reduce-scatter.15
  525.9 58.9 reduce-scatter.19
  587.7 56.2 all-gather.19
  646.5 87.1 all-reduce.8
  736.5 141.5 reduce-scatter.13
  880.9 138.6 reduce-scatter.9
  1022.2 138.4 reduce-scatter.7
  1163.4 138.4 reduce-scatter.11
